TPU v7x, 32 devices: a whole 2x2x4 slice. The times are simulated.
32 devices in a mesh: dp: 8 (over z, x), tensor: 4 (over y, core).
Axes of the slice: x: 2, y: 2, z: 4, core: 2. Of those that a mesh axis runs over, the one named last changes fastest.
Arguments:
- residual_in: float32 [16384, 768], P(('dp', 'tensor')), may hold values from -6 to 6
- out_grad: float32 [16384, 768], P(('dp', 'tensor')), may hold values from -6 to 6
- seq_lengths: int32 [8, 16], P('dp'), may hold values from 0 to 1024, as said below
- timesteps: int32 [8, 16], P('dp'), may hold values from 0 to 1023
- norm_gain: float32 [768], replicated, may hold values from 0.5 to 1.5
- norm_bias: float32 [768], replicated, may hold values from -3 to 3
- qkv_weight: float32 [3, 768, 768], P(None, 'dp', 'tensor'), may hold values from -0.21875 to 0.21875
- proj_weight: float32 [768, 768], P('tensor', 'dp'), may hold values from -0.875 to 0.875
- proj_bias: float32 [768], replicated, may hold values from -2 to 2
- up_weight: float32 [768, 3072], P('dp', 'tensor'), may hold values from -0.21875 to 0.21875
- up_bias: float32 [3072], replicated, may hold values from -3 to 3
- down_weight: float32 [3072, 768], P('tensor', 'dp'), may hold values from -0.109375 to 0.109375
- down_bias: float32 [768], replicated, may hold values from -2 to 2
- time_weight: float32 [128, 2304], replicated, may hold values from -0.5 to 0.5
- time_bias: float32 [2304], replicated, may hold values from -3 to 3
Outputs:
- residual_out: float32 [16384, 768], P(('dp', 'tensor'))
- input_grad: float32 [16384, 768], P(('dp', 'tensor'))
- norm_gain_grad: float32 [768], replicated
- norm_bias_grad: float32 [768], replicated
- qkv_weight_grad: float32 [3, 768, 768], P(None, 'dp', 'tensor')
- proj_weight_grad: float32 [768, 768], P('tensor', 'dp')
- proj_bias_grad: float32 [768], replicated
- up_weight_grad: float32 [768, 3072], P('dp', 'tensor')
- up_bias_grad: float32 [3072], replicated
- down_weight_grad: float32 [3072, 768], P('tensor', 'dp')
- down_bias_grad: float32 [768], replicated
- time_weight_grad: float32 [128, 2304], replicated
- time_bias_grad: float32 [2304], replicated
Inputs may be any that keep to these rules, and one draw needn't show every extreme that they name: `seq_lengths`: row g lists the lengths of the sequences packed in order into the 2048 rows of pack g: the nonzero lengths come first and lie between 128 and 1024, their sum is at most 2048, the rows after it are padding, and every row holds a length of exactly 1024.
All inputs are finite; a program needn't handle non-finite values.
Results may differ from a plain program's by a relative error of at most 0.015.
Values may be sent and summed in bfloat16 or wider, within the bound.
A program may use at most 128 MiB of HBM per device.

v0:
```python
import math
import jax
import jax.numpy as jnp
from jax import lax
from jax.sharding import PartitionSpec as P

HDIM = 64
QBLK = 512
highest = lax.Precision.HIGHEST


def normalize(values):
    center = values - jnp.mean(values, axis=-1, keepdims=True)
    inverse = lax.rsqrt(jnp.mean(center * center, axis=-1, keepdims=True) + 1e-05)
    return (center * inverse, inverse)


def norm_back(grad_in, normed, inverse):
    return inverse * (
        grad_in
        - jnp.mean(grad_in, axis=-1, keepdims=True)
        - normed * jnp.mean(grad_in * normed, axis=-1, keepdims=True)
    )


def pack_info(lengths, row_total):
    row_index = jnp.arange(row_total, dtype=jnp.int32)
    seq_ends = jnp.cumsum(lengths)
    passed = row_index[:, None] >= seq_ends[None, :]
    segment = jnp.sum(passed.astype(jnp.int32), axis=1)
    starts = jnp.sum(jnp.where(passed, lengths[None, :], 0), axis=1)
    return (segment, row_index - starts)


def time_embed(time_index, embed_width):
    half_width = embed_width // 2
    freqs = jnp.exp(-math.log(10000.0) * jnp.arange(half_width, dtype=jnp.float32) / half_width)
    angles = time_index.astype(jnp.float32)[:, None] * freqs[None, :]
    return jnp.concatenate([jnp.cos(angles), jnp.sin(angles)], axis=1)


def rope_tables(positions, head_width):
    half_width = head_width // 2
    inverse = jnp.exp(
        -math.log(10000.0) * jnp.arange(half_width, dtype=jnp.float32) * (2.0 / head_width)
    )
    angles = positions.astype(jnp.float32)[:, None] * inverse[None, :]
    return (jnp.cos(angles)[:, None, :], jnp.sin(angles)[:, None, :])


def rotate(values, cosine, sine_table):
    half_width = values.shape[-1] // 2
    lead_half = values[..., :half_width]
    tail_half = values[..., half_width:]
    return jnp.concatenate(
        [lead_half * cosine - tail_half * sine_table, tail_half * cosine + lead_half * sine_table],
        axis=-1,
    )


def masked_scores(query_block, segment_block, keys_low, segment):
    scores = jnp.einsum("qhd,khd->hqk", query_block, keys_low, preferred_element_type=jnp.float32)
    allowed = segment_block[:, None] == segment[None, :]
    return jnp.where(allowed[None], scores, -1000000000.0)


def gelu_tanh(values):
    return jax.nn.gelu(values, approximate=True)


def shards(
    residual_in,
    out_grad,
    seq_lengths,
    timesteps,
    norm_gain,
    norm_bias,
    qkv_weight,
    proj_weight,
    proj_bias,
    up_weight,
    up_bias,
    down_weight,
    down_bias,
    time_weight,
    time_bias,
):
    row_count = residual_in.shape[0]
    width_model = residual_in.shape[1]
    tensor_size = lax.axis_size("tensor")
    tensor_rank = lax.axis_index("tensor")
    total_rows = row_count * tensor_size
    own_offset = tensor_rank * row_count
    segment, positions = pack_info(seq_lengths[0], total_rows)
    slot_count = seq_lengths.shape[1]
    own_segment = lax.dynamic_slice_in_dim(segment, own_offset, row_count)
    onehot = (own_segment[:, None] == jnp.arange(slot_count, dtype=jnp.int32)[None, :]).astype(
        jnp.float32
    )
    embedded = time_embed(timesteps[0], time_weight.shape[0])
    mod_table = jnp.dot(embedded, time_weight, precision=highest) + time_bias
    modulation = jnp.dot(onehot, mod_table, precision=highest)
    mod_scale = modulation[:, :width_model]
    mod_shift = modulation[:, width_model : 2 * width_model]
    mod_gate = modulation[:, 2 * width_model :]
    gathered_qkv, gathered_proj, gathered_up, gathered_down = (
        lax.all_gather(qkv_weight.astype(jnp.bfloat16), "dp", axis=1, tiled=True),
        lax.all_gather(proj_weight.astype(jnp.bfloat16), "dp", axis=1, tiled=True),
        lax.all_gather(up_weight.astype(jnp.bfloat16), "dp", axis=0, tiled=True),
        lax.all_gather(down_weight.astype(jnp.bfloat16), "dp", axis=1, tiled=True),
    )
    local_heads = gathered_qkv.shape[2] // HDIM
    local_units = gathered_up.shape[1]
    normed_in, inverse_in = normalize(residual_in)
    normed_low = (normed_in * norm_gain + norm_bias).astype(jnp.bfloat16)
    normed_full = lax.all_gather(normed_low, "tensor", axis=0, tiled=True)
    projected = jnp.einsum(
        "td,cde->cte", normed_full, gathered_qkv, preferred_element_type=jnp.float32
    )
    cosine, sine_table = rope_tables(positions, HDIM)
    head_scale = 1.0 / math.sqrt(HDIM)
    queries_low = (
        rotate(projected[0].reshape(total_rows, local_heads, HDIM), cosine, sine_table) * head_scale
    ).astype(jnp.bfloat16)
    keys_low = rotate(
        projected[1].reshape(total_rows, local_heads, HDIM), cosine, sine_table
    ).astype(jnp.bfloat16)
    values_low = projected[2].reshape(total_rows, local_heads, HDIM).astype(jnp.bfloat16)
    block_count = total_rows // QBLK
    query_blocks = queries_low.reshape(block_count, QBLK, local_heads, HDIM)
    segment_blocks = segment.reshape(block_count, QBLK)

    def forward_block(block_item):
        query_block, segment_block = block_item
        scores = masked_scores(query_block, segment_block, keys_low, segment)
        row_max = jnp.max(scores, axis=-1, keepdims=True)
        exponent = jnp.exp(scores - row_max)
        row_total = jnp.sum(exponent, axis=-1, keepdims=True)
        soft_weights = exponent / row_total
        mixed = jnp.einsum(
            "hqk,khd->qhd",
            soft_weights.astype(jnp.bfloat16),
            values_low,
            preferred_element_type=jnp.float32,
        )
        return (mixed.astype(jnp.bfloat16), (row_max + jnp.log(row_total))[..., 0])

    mixed_blocks, log_totals = lax.map(forward_block, (query_blocks, segment_blocks))
    mixed_flat = mixed_blocks.reshape(total_rows, local_heads * HDIM)
    attention = lax.psum_scatter(
        jnp.dot(mixed_flat, gathered_proj, preferred_element_type=jnp.float32).astype(jnp.bfloat16),
        "tensor",
        scatter_dimension=0,
        tiled=True,
    ).astype(jnp.float32)
    hidden = residual_in + attention + proj_bias
    hidden_normed, inverse_hidden = normalize(hidden)
    modulated_low = (hidden_normed * (1.0 + mod_scale) + mod_shift).astype(jnp.bfloat16)
    branch_grad = out_grad * mod_gate
    modulated_full = lax.all_gather(modulated_low, "tensor", axis=0, tiled=True)
    up_bias_own = lax.dynamic_slice_in_dim(up_bias, tensor_rank * local_units, local_units)
    pre_act = jnp.dot(modulated_full, gathered_up, preferred_element_type=jnp.float32) + up_bias_own
    active, gelu_pullback = jax.vjp(gelu_tanh, pre_act)
    active_low = active.astype(jnp.bfloat16)
    down_sum = lax.psum_scatter(
        jnp.dot(active_low, gathered_down, preferred_element_type=jnp.float32).astype(jnp.bfloat16),
        "tensor",
        scatter_dimension=0,
        tiled=True,
    ).astype(jnp.float32)
    branch = down_sum + down_bias
    residual_out = hidden + mod_gate * branch
    gate_grad = out_grad * branch
    branch_full = lax.all_gather(branch_grad.astype(jnp.bfloat16), "tensor", axis=0, tiled=True)
    down_part = lax.dot_general(
        active_low, branch_full, (((0,), (0,)), ((), ())), preferred_element_type=jnp.float32
    )
    active_grad = lax.dot_general(
        branch_full, gathered_down, (((1,), (1,)), ((), ())), preferred_element_type=jnp.float32
    )
    pre_grad = gelu_pullback(active_grad)[0].astype(jnp.bfloat16)
    up_bias_own_part = jnp.sum(pre_grad, axis=0, dtype=jnp.float32)
    up_bias_part = lax.dynamic_update_slice_in_dim(
        jnp.zeros(up_bias.shape, jnp.float32), up_bias_own_part, tensor_rank * local_units, 0
    )
    up_part = lax.dot_general(
        modulated_full, pre_grad, (((0,), (0,)), ((), ())), preferred_element_type=jnp.float32
    )
    modulated_grad = lax.psum_scatter(
        lax.dot_general(
            pre_grad, gathered_up, (((1,), (1,)), ((), ())), preferred_element_type=jnp.float32
        ).astype(jnp.bfloat16),
        "tensor",
        scatter_dimension=0,
        tiled=True,
    ).astype(jnp.float32)
    down_bias_part = jnp.sum(branch_grad, axis=0)
    scale_grad = modulated_grad * hidden_normed
    hidden_norm_grad = modulated_grad * (1.0 + mod_scale)
    hidden_grad = out_grad + norm_back(hidden_norm_grad, hidden_normed, inverse_hidden)
    mod_grad = jnp.concatenate([scale_grad, modulated_grad, gate_grad], axis=1)
    mod_seq_grad = lax.dot_general(onehot, mod_grad, (((0,), (0,)), ((), ())), precision=highest)
    time_weight_part = lax.dot_general(
        embedded, mod_seq_grad, (((0,), (0,)), ((), ())), precision=highest
    )
    time_bias_part = jnp.sum(mod_seq_grad, axis=0)
    proj_bias_part = jnp.sum(hidden_grad, axis=0)
    hidden_full = lax.all_gather(hidden_grad.astype(jnp.bfloat16), "tensor", axis=0, tiled=True)
    proj_part = lax.dot_general(
        mixed_flat, hidden_full, (((0,), (0,)), ((), ())), preferred_element_type=jnp.float32
    )
    mixed_grad = lax.dot_general(
        hidden_full, gathered_proj, (((1,), (1,)), ((), ())), preferred_element_type=jnp.float32
    )
    grad_blocks = mixed_grad.astype(jnp.bfloat16).reshape(block_count, QBLK, local_heads, HDIM)

    def backward_block(carried, block_item):
        key_sum, value_sum = carried
        query_block, segment_block, log_block, grad_block = block_item
        scores = masked_scores(query_block, segment_block, keys_low, segment)
        soft_weights = jnp.exp(scores - log_block[:, :, None])
        prob_grad = jnp.einsum(
            "qhd,khd->hqk", grad_block, values_low, preferred_element_type=jnp.float32
        )
        row_inner = jnp.sum(soft_weights * prob_grad, axis=-1, keepdims=True)
        score_grad = (soft_weights * (prob_grad - row_inner)).astype(jnp.bfloat16)
        query_grad = jnp.einsum(
            "hqk,khd->qhd", score_grad, keys_low, preferred_element_type=jnp.float32
        )
        key_sum = key_sum + jnp.einsum(
            "hqk,qhd->khd", score_grad, query_block, preferred_element_type=jnp.float32
        )
        value_sum = value_sum + jnp.einsum(
            "hqk,qhd->khd",
            soft_weights.astype(jnp.bfloat16),
            grad_block,
            preferred_element_type=jnp.float32,
        )
        return ((key_sum, value_sum), query_grad)

    empty_grad = jnp.zeros((total_rows, local_heads, HDIM), jnp.float32)
    (key_grad, value_grad), query_grads = lax.scan(
        backward_block,
        (empty_grad, empty_grad),
        (query_blocks, segment_blocks, log_totals, grad_blocks),
    )
    query_grad_all = query_grads.reshape(total_rows, local_heads, HDIM)
    query_raw_grad = rotate(query_grad_all * head_scale, cosine, -sine_table)
    key_raw_grad = rotate(key_grad, cosine, -sine_table)
    qkv_grad = (
        jnp.stack([query_raw_grad, key_raw_grad, value_grad])
        .reshape(3, total_rows, local_heads * HDIM)
        .astype(jnp.bfloat16)
    )
    qkv_part = jnp.einsum("td,cte->cde", normed_full, qkv_grad, preferred_element_type=jnp.float32)
    normed_grad = lax.psum_scatter(
        jnp.einsum(
            "cte,cde->td", qkv_grad, gathered_qkv, preferred_element_type=jnp.float32
        ).astype(jnp.bfloat16),
        "tensor",
        scatter_dimension=0,
        tiled=True,
    ).astype(jnp.float32)
    gain_part = jnp.sum(normed_grad * normed_in, axis=0)
    bias_part = jnp.sum(normed_grad, axis=0)
    input_grad = hidden_grad + norm_back(normed_grad * norm_gain, normed_in, inverse_in)
    grad_qkv, grad_proj, grad_up, grad_down = (
        lax.psum_scatter(qkv_part, "dp", scatter_dimension=1, tiled=True),
        lax.psum_scatter(proj_part, "dp", scatter_dimension=1, tiled=True),
        lax.psum_scatter(up_part, "dp", scatter_dimension=0, tiled=True),
        lax.psum_scatter(down_part, "dp", scatter_dimension=1, tiled=True),
    )
    small_sums = lax.psum(
        (
            gain_part,
            bias_part,
            proj_bias_part,
            up_bias_part,
            down_bias_part,
            time_weight_part,
            time_bias_part,
        ),
        ("dp", "tensor"),
    )
    return (
        residual_out,
        input_grad,
        small_sums[0],
        small_sums[1],
        grad_qkv,
        grad_proj,
        small_sums[2],
        grad_up,
        small_sums[3],
        grad_down,
        small_sums[4],
        small_sums[5],
        small_sums[6],
    )


def solution(mesh):
    in_specs = (
        P(("dp", "tensor"), None),
        P(("dp", "tensor"), None),
        P("dp", None),
        P("dp", None),
        P(),
        P(),
        P(None, "dp", "tensor"),
        P("tensor", "dp"),
        P(),
        P("dp", "tensor"),
        P(),
        P("tensor", "dp"),
        P(),
        P(),
        P(),
    )
    out_specs = (
        P(("dp", "tensor"), None),
        P(("dp", "tensor"), None),
        P(),
        P(),
        P(None, "dp", "tensor"),
        P("tensor", "dp"),
        P(),
        P("dp", "tensor"),
        P(),
        P("tensor", "dp"),
        P(),
        P(),
        P(),
    )
    return jax.shard_map(shards, mesh=mesh, in_specs=in_specs, out_specs=out_specs, check_vma=False)
```

profile of v0, /device:TPU:0, one launch (start us, length us, event | category | flops | bytes accessed | tf_op | source)
XLA Modules:
  0.0 983.2 jit_solution(7752783415744753247)
XLA Ops:
  12.9 40.6 %all_gather.25 = bf16[3,768,192]{2,0,1:T(4,128)(2,1)} all-gather(bf16[3,96,192]{2,0,1:T(4,128)(2,1)S(1)} %copy.65), channel_id=1, replica_groups=mesh['dp'=8,'tensor'=4] {'dp'}, dimensions={1}, use_global_device_ids=true | all-gather | bytes 995328 | tf_op jit(solution)/shard_map/all_gather | solution.py:107
  57.0 33.0 %all_gather.26 = bf16[192,768]{0,1:T(8,128)(2,1)} all-gather(bf16[192,96]{0,1:T(8,128)(2,1)S(1)} %copy.69), channel_id=1, replica_groups=mesh['dp'=8,'tensor'=4] {'dp'}, dimensions={1}, use_global_device_ids=true | all-gather | bytes 331776 | tf_op jit(solution)/shard_map/all_gather | solution.py:108
  91.7 4.2 fusion.87
  106.1 95.3 %while.27 = (s32[]{:T(128)}, bf16[4,512,3,64]{1,3,2,0:T(8,128)(2,1)}, f32[4,3,512]{2,1,0:T(4,128)}, s32[4,512]{1,0:T(4,128)S(1)}, s32[2048]{0:T(1024)S(1)}, /*in...) while((s32[]{:T(128)}, ...), condition=%wide.region_8.9_spmd, body=%wide.region_5.8_spmd.sunk | while | flops 834763264 | bytes 47120528 | solution.py:148
  107.0 7.6 select_reduce_fusion.3
  114.6 7.8 fusion.140
  122.4 7.1 fusion.141
  130.7 7.6 select_reduce_fusion.3
  138.3 7.8 fusion.140
  146.1 7.1 fusion.141
  154.5 7.6 select_reduce_fusion.3
  162.1 7.8 fusion.140
  169.9 7.1 fusion.141
  178.2 7.6 select_reduce_fusion.3
  185.8 7.8 fusion.140
  193.7 7.1 fusion.141
  213.7 4.3 fusion.71
  218.0 26.7 %reduce-scatter.13.cloned.1.call-done = bf16[512,768]{1,0:T(8,128)(2,1)} async-done(((bf16[2048,768]{1,0:T(8,128)(2,1)}), bf16[512,768]{1,0:T(8,128)(2,1)}) %reduce-scatter.13.cloned.1.call-update) | async-done | bytes 786448 | tf_op jit(solution)/shard_map/reduce_scatter | solution.py:150
  252.9 27.2 %all-gather.9.cloned.1.call-done = bf16[2048,768]{1,0:T(8,128)(2,1)} async-done(((bf16[512,768]{1,0:T(8,128)(2,1)}), bf16[2048,768]{1,0:T(8,128)(2,1)}) %all-gather.9.cloned.1.call-update) | async-done | bytes 3145744 | tf_op jit(solution)/shard_map/all_gather | solution.py:160
  280.1 7.5 fusion.88
  287.6 36.0 %all-gather.13.cloned.1.call-done = bf16[768,768]{0,1:T(8,128)(2,1)} async-done(((bf16[768,96]{0,1:T(8,128)(2,1)}), bf16[768,768]{0,1:T(8,128)(2,1)}) %all-gather.13.cloned.1.call-update) | async-done | bytes 1179664 | tf_op jit(solution)/shard_map/all_gather | solution.py:110
  323.6 28.9 %all-gather.15.cloned.1.call-done = bf16[2048,768]{1,0:T(8,128)(2,1)} async-done(((bf16[512,768]{1,0:T(8,128)(2,1)}), bf16[2048,768]{1,0:T(8,128)(2,1)}) %all-gather.15.cloned.1.call-update) | async-done | bytes 3145744 | tf_op jit(solution)/shard_map/all_gather | solution.py:174
  352.6 10.8 %convert_reduce_fusion = (f32[768]{0:T(1024)}, bf16[2048,768]{1,0:T(8,128)(2,1)S(1)}, bf16[2048,768]{1,0:T(8,128)(2,1)}) fusion(f32[2048,768]{1,0:T(8,128)} %fusion.88, f32[768]{0:T(1024)S(1)} %dynamic_slice.28, bf16[2048,768]{1,0:T(8,128)(2,1)} %all-gather.15.cloned.1.call-done, bf16[768,768]{0,1:T(8,128)(2,1)} %all-gather.13.cloned.1.call-done), kind=kOutput, calls=%fused_computation.57 | convolution fusion | flops 2455239936 | bytes 16914432 | tf_op jit(solution)/shard_map/dot_general | solution.py:178
  365.1 4.0 convolution_convert_fusion
  370.3 6.2 convolution_convert_fusion.1
  376.6 30.5 %reduce-scatter.17.cloned.1.call-done = bf16[512,768]{1,0:T(8,128)(2,1)} async-done(((bf16[2048,768]{1,0:T(8,128)(2,1)}), bf16[512,768]{1,0:T(8,128)(2,1)}) %reduce-scatter.17.cloned.1.call-update) | async-done | bytes 786448 | tf_op jit(solution)/shard_map/reduce_scatter | solution.py:189
  407.1 3.9 fusion.72
  411.1 36.4 %reduce-scatter.15.cloned.1.call-done = bf16[512,768]{1,0:T(8,128)(2,1)} async-done(((bf16[2048,768]{1,0:T(8,128)(2,1)}), bf16[512,768]{1,0:T(8,128)(2,1)}) %reduce-scatter.15.cloned.1.call-update) | async-done | bytes 786448 | tf_op jit(solution)/shard_map/reduce_scatter | solution.py:165
  447.4 5.1 fusion.83
  454.8 28.4 %all-gather.17.cloned.1.call-done = bf16[2048,768]{1,0:T(8,128)(2,1)} async-done(((bf16[512,768]{1,0:T(8,128)(2,1)}), bf16[2048,768]{1,0:T(8,128)(2,1)}) %all-gather.17.cloned.1.call-update) | async-done | bytes 3145744 | tf_op jit(solution)/shard_map/all_gather | solution.py:208
  487.0 157.7 %while.28 = (s32[]{:T(128)}, f32[2048,3,64]{0,2,1:T(8,128)}, f32[2048,3,64]{0,2,1:T(8,128)}, f32[4,512,3,64]{1,0,3,2:T(4,128)}, bf16[4,512,3,64]{1,3,2,0:T(8,128...) while((s32[]{:T(128)}, f32[2048,3,64]{0,2,1:T(8,128)}, ...), condition=%wide.region_18.19_spmd.clone, body=%wide.region_16.18_spmd.clone.sunk | while | flops 2053634560 | bytes 151972176 | solution.py:242
  491.6 4.4 fusion.153
  496.0 5.4 multiply_reduce_fusion.5
  501.4 5.9 multiply_convert_fusion.3
  507.3 5.1 convolution_bitcast_fusion.4
  516.4 8.6 dynamic_update_slice.24
  529.5 5.8 fusion.153
  535.3 5.4 multiply_reduce_fusion.5
  540.7 5.9 multiply_convert_fusion.3
  546.6 5.1 convolution_bitcast_fusion.4
  551.7 4.1 fusion.152
  556.3 8.6 dynamic_update_slice.24
  569.3 5.8 fusion.153
  575.1 5.4 multiply_reduce_fusion.5
  580.5 5.9 multiply_convert_fusion.3
  586.4 5.1 convolution_bitcast_fusion.4
  591.6 4.1 fusion.152
  596.1 8.6 dynamic_update_slice.24
  609.2 5.8 fusion.153
  614.9 5.4 multiply_reduce_fusion.5
  620.4 5.9 multiply_convert_fusion.3
  626.2 5.1 convolution_bitcast_fusion.4
  631.4 4.1 fusion.152
  635.9 8.6 dynamic_update_slice.24
  647.6 4.5 convolution_bitcast_fusion.2
  668.3 5.7 bitcast_convert_fusion
  675.9 6.0 fusion.89
  682.2 6.9 fusion.90
  696.3 19.6 %reduce-scatter.27.cloned.1.call-done = f32[96,192]{1,0:T(8,128)} async-done(((f32[768,192]{1,0:T(8,128)}), f32[96,192]{1,0:T(8,128)}) %reduce-scatter.27.cloned.1.call-update) | async-done | bytes 73744
  717.5 68.3 %reduce-scatter.25.cloned.1.call-done = f32[96,576]{1,0:T(8,128)} async-done(((f32[768,576]{1,0:T(8,128)}), f32[96,576]{1,0:T(8,128)}) %reduce-scatter.25.cloned.1.call-update) | async-done | bytes 221200
  787.7 37.6 %reduce-scatter.19.cloned.1.call-done = bf16[512,768]{1,0:T(8,128)(2,1)} async-done(((bf16[2048,768]{1,0:T(8,128)(2,1)}), bf16[512,768]{1,0:T(8,128)(2,1)}) %reduce-scatter.19.cloned.1.call-update) | async-done | bytes 786448 | tf_op jit(solution)/shard_map/reduce_scatter | solution.py:256
  827.8 41.3 %all-reduce = (f32[768]{0:T(1024)}, f32[768]{0:T(1024)}, f32[768]{0:T(1024)}, f32[3072]{0:T(1024)}, f32[768]{0:T(1024)}, /*index=5*/f32[2304]{0:T(1024)}) all-reduce(f32[768]{0:T(1024)S(1)} %get-tuple-element.311, f32[768]{0:T(1024)S(1)} %get-tuple-element.314, ...), channel_id=1, replica_groups=mesh['dp'=8,'tensor'=4] {'dp','tensor'}, use_global_device_ids=true, to_apply=%region_23.24 | all-reduce | flops 8448 | bytes 67584 | tf_op jit(solution)/shard_map/psum | solution.py:273
  872.3 27.9 %reduce-scatter.21.cloned.1.call-done = f32[96,768]{1,0:T(8,128)} async-done(((f32[768,768]{1,0:T(8,128)}), f32[96,768]{1,0:T(8,128)}) %reduce-scatter.21.cloned.1.call-update) | async-done | bytes 294928 | tf_op jit(solution)/shard_map/reduce_scatter | solution.py:270
  900.2 73.0 %reduce-scatter.23.cloned.1.call-done = f32[768,96]{0,1:T(8,128)} async-done(((f32[768,768]{0,1:T(8,128)}), f32[768,96]{0,1:T(8,128)}) %reduce-scatter.23.cloned.1.call-update) | async-done | bytes 294928 | tf_op jit(solution)/shard_map/reduce_scatter | solution.py:271
  (301 shorter events, 117.1 us)
Async XLA Ops:
  8.0 204.3 %copy-start = (f32[128,2304]{1,0:T(8,128)S(1)}, f32[128,2304]{1,0:T(8,128)}, u32[]{:S(2)}) copy-start(f32[128,2304]{1,0:T(8,128)} %param.32) | copy-start | bytes 3538948
  8.1 83.6 %all-gather.7.cloned.1.call-start = ((), (), s32[]{:S(2)}) async-start(), calls=%async_computation.8 | async-start | bytes 3932160 | tf_op jit(solution)/shard_map/all_gather | solution.py:116
  11.6 233.2 %reduce-scatter.13.cloned.1.call-start = ((), (), s32[]{:S(2)}) async-start(), calls=%async_computation.9 | async-start | bytes 3932160 | tf_op jit(solution)/shard_map/reduce_scatter | solution.py:150
  53.5 36.4 %copy-start.45 = (s32[2048]{0:T(1024)S(1)}, s32[2048]{0:T(1024)}, u32[]{:S(2)}) copy-start(s32[2048]{0:T(1024)} %get-tuple-element.315) | copy-start | bytes 24580
  91.7 5.6 copy-start.22
  114.6 7.8 copy-start.10
  138.3 7.8 copy-start.10
  162.1 7.8 copy-start.10
  185.8 7.8 copy-start.10
  206.9 46.0 %all-gather.11.cloned.1.call-start = ((), (), s32[]{:S(2)}) async-start(), calls=%async_computation.11 | async-start | bytes 1327104 | tf_op jit(solution)/shard_map/all_gather | solution.py:109
  208.6 71.5 %all-gather.9.cloned.1.call-start = ((), (), s32[]{:S(2)}) async-start(), calls=%async_computation.10 | async-start | bytes 3932160 | tf_op jit(solution)/shard_map/all_gather | solution.py:160
  213.7 31.1 %copy-start.52 = (f32[768]{0:T(1024)S(1)}, f32[768]{0:T(1024)}, u32[]{:S(2)}) copy-start(f32[768]{0:T(1024)} %param.27) | copy-start | bytes 9220
  246.3 4.2 copy-start.11
  247.5 3.1 copy-start.33
  250.6 73.1 %all-gather.13.cloned.1.call-start = ((), (), s32[]{:S(2)}) async-start(), calls=%async_computation.12 | async-start | bytes 1327104 | tf_op jit(solution)/shard_map/all_gather | solution.py:110
  251.3 101.2 %all-gather.15.cloned.1.call-start = ((), (), s32[]{:S(2)}) async-start(), calls=%async_computation.14 | async-start | bytes 3932160 | tf_op jit(solution)/shard_map/all_gather | solution.py:174
  252.1 155.1 %reduce-scatter.17.cloned.1.call-start = ((), (), s32[]{:S(2)}) async-start(), calls=%async_computation.15 | async-start | bytes 3932160 | tf_op jit(solution)/shard_map/reduce_scatter | solution.py:189
  287.6 77.4 %copy-start.57 = (bf16[768,768]{1,0:T(8,128)(2,1)S(1)}, bf16[768,768]{1,0:T(8,128)(2,1)}, u32[]{:S(2)}) copy-start(bf16[768,768]{1,0:T(8,128)(2,1)} %all-gather.11.cloned.1.call-done) | copy-start | bytes 3538948
  369.1 78.3 %reduce-scatter.15.cloned.1.call-start = ((), (), s32[]{:S(2)}) async-start(), calls=%async_computation.13 | async-start | bytes 3932160 | tf_op jit(solution)/shard_map/reduce_scatter | solution.py:165
  376.6 30.6 %copy-start.12 = (f32[512,768]{1,0:T(8,128)S(1)}, f32[512,768]{1,0:T(8,128)}, u32[]{:S(2)}) copy-start(f32[512,768]{1,0:T(8,128)} %copy-done.11) | copy-start | bytes 4718596
  376.6 70.9 %copy-start.53 = (f32[768]{0:T(1024)S(1)}, f32[768]{0:T(1024)}, u32[]{:S(2)}) copy-start(f32[768]{0:T(1024)} %param.31) | copy-start | bytes 9220
  376.6 106.6 %all-gather.17.cloned.1.call-start = ((), (), s32[]{:S(2)}) async-start(), calls=%async_computation.16 | async-start | bytes 3932160 | tf_op jit(solution)/shard_map/all_gather | solution.py:208
  407.1 40.3 %copy-start.16 = (bf16[512,768]{1,0:T(8,128)(2,1)S(1)}, bf16[512,768]{1,0:T(8,128)(2,1)}, u32[]{:S(2)}) copy-start(bf16[512,768]{1,0:T(8,128)(2,1)} %reduce-scatter.17.cloned.1.call-done) | copy-start | bytes 2359300
  452.5 30.6 %copy-start.19 = (bf16[192,768]{0,1:T(8,128)(2,1)S(1)}, bf16[192,768]{0,1:T(8,128)(2,1)}, u32[]{:S(2)}) copy-start(bf16[192,768]{0,1:T(8,128)(2,1)} %all_gather.26) | copy-start | bytes 884740
  454.7 261.2 %reduce-scatter.27.cloned.1.call-start = ((), (), s32[]{:S(2)}) async-start(), calls=%async_computation.22 | async-start | bytes 884736
  487.2 4.5 copy-start.4
  487.2 4.5 copy-start.14
  488.6 3.0 copy-start.3
  507.3 5.1 copy-start.2
  512.4 12.6 %copy-start.5 = (bf16[2048,3,64]{0,2,1:T(8,128)(2,1)S(1)}, bf16[2048,3,64]{0,2,1:T(8,128)(2,1)}, u32[]{:S(2)}) copy-start(bf16[2048,3,64]{0,2,1:T(8,128)(2,1)} %copy-done.4) | copy-start | bytes 2359300 | tf_op jit(solution)/shard_map/while
  512.5 12.6 %copy-start.15 = (bf16[4,512,3,64]{1,3,2,0:T(8,128)(2,1)S(1)}, bf16[4,512,3,64]{1,3,2,0:T(8,128)(2,1)}, u32[]{:S(2)}) copy-start(bf16[4,512,3,64]{1,3,2,0:T(8,128)(2,1)} %copy-done.14) | copy-start | bytes 2359300 | tf_op jit(solution)/shard_map/while
  525.0 4.4 copy-start.4
  525.0 4.4 copy-start.14
  526.5 3.0 copy-start.3
  546.6 5.1 copy-start.2
  551.7 13.2 %copy-start.5 = (bf16[2048,3,64]{0,2,1:T(8,128)(2,1)S(1)}, bf16[2048,3,64]{0,2,1:T(8,128)(2,1)}, u32[]{:S(2)}) copy-start(bf16[2048,3,64]{0,2,1:T(8,128)(2,1)} %copy-done.4) | copy-start | bytes 2359300 | tf_op jit(solution)/shard_map/while
  551.7 13.1 %copy-start.15 = (bf16[4,512,3,64]{1,3,2,0:T(8,128)(2,1)S(1)}, bf16[4,512,3,64]{1,3,2,0:T(8,128)(2,1)}, u32[]{:S(2)}) copy-start(bf16[4,512,3,64]{1,3,2,0:T(8,128)(2,1)} %copy-done.14) | copy-start | bytes 2359300 | tf_op jit(solution)/shard_map/while
  564.9 4.4 copy-start.4
  564.9 4.4 copy-start.14
  586.4 5.1 copy-start.2
  591.5 13.2 %copy-start.5 = (bf16[2048,3,64]{0,2,1:T(8,128)(2,1)S(1)}, bf16[2048,3,64]{0,2,1:T(8,128)(2,1)}, u32[]{:S(2)}) copy-start(bf16[2048,3,64]{0,2,1:T(8,128)(2,1)} %copy-done.4) | copy-start | bytes 2359300 | tf_op jit(solution)/shard_map/while
  591.5 13.1 %copy-start.15 = (bf16[4,512,3,64]{1,3,2,0:T(8,128)(2,1)S(1)}, bf16[4,512,3,64]{1,3,2,0:T(8,128)(2,1)}, u32[]{:S(2)}) copy-start(bf16[4,512,3,64]{1,3,2,0:T(8,128)(2,1)} %copy-done.14) | copy-start | bytes 2359300 | tf_op jit(solution)/shard_map/while
  604.7 4.4 copy-start.4
  604.7 4.4 copy-start.14
  626.2 5.1 copy-start.2
  631.4 13.2 %copy-start.5 = (bf16[2048,3,64]{0,2,1:T(8,128)(2,1)S(1)}, bf16[2048,3,64]{0,2,1:T(8,128)(2,1)}, u32[]{:S(2)}) copy-start(bf16[2048,3,64]{0,2,1:T(8,128)(2,1)} %copy-done.4) | copy-start | bytes 2359300 | tf_op jit(solution)/shard_map/while
  631.4 13.1 %copy-start.15 = (bf16[4,512,3,64]{1,3,2,0:T(8,128)(2,1)S(1)}, bf16[4,512,3,64]{1,3,2,0:T(8,128)(2,1)}, u32[]{:S(2)}) copy-start(bf16[4,512,3,64]{1,3,2,0:T(8,128)(2,1)} %copy-done.14) | copy-start | bytes 2359300 | tf_op jit(solution)/shard_map/while
  647.6 4.6 copy-start.6
  647.6 4.6 copy-start.23
  652.1 133.7 %reduce-scatter.25.cloned.1.call-start = ((), (), s32[]{:S(2)}) async-start(), calls=%async_computation.21 | async-start | bytes 2211840
  666.9 158.4 %reduce-scatter.19.cloned.1.call-start = ((), (), s32[]{:S(2)}) async-start(), calls=%async_computation.17 | async-start | bytes 3932160 | tf_op jit(solution)/shard_map/reduce_scatter | solution.py:256
  674.0 226.3 %reduce-scatter.21.cloned.1.call-start = ((), (), s32[]{:S(2)}) async-start(), calls=%async_computation.18 | async-start | bytes 2654208 | tf_op jit(solution)/shard_map/reduce_scatter | solution.py:270
  681.9 291.4 %reduce-scatter.23.cloned.1.call-start = ((), (), s32[]{:S(2)}) async-start(), calls=%async_computation.19 | async-start | bytes 2654208 | tf_op jit(solution)/shard_map/reduce_scatter | solution.py:271
  689.2 284.1 %all-reduce.3.cloned.1.call-start = ((), (), s32[]{:S(2)}) async-start(), calls=%async_computation.20 | async-start | bytes 2359296 | tf_op jit(solution)/shard_map/psum | solution.py:273
  690.8 3.1 copy-start.36
  690.8 3.1 copy-start.38
  694.0 131.3 %copy-start.8 = (f32[512,768]{1,0:T(8,128)S(1)}, f32[512,768]{1,0:T(8,128)}, u32[]{:S(2)}) copy-start(f32[512,768]{1,0:T(8,128)} %param.19) | copy-start | bytes 4718596
  694.0 131.3 %copy-start.40 = (f32[512]{0:T(512)S(1)}, f32[512]{0:T(512)}, u32[]{:S(2)}) copy-start(f32[512]{0:T(512)} %copy-done.39) | copy-start | bytes 6148
  694.0 131.2 %copy-start.42 = (f32[768]{0:T(1024)S(1)}, f32[768]{0:T(1024)}, u32[]{:S(2)}) copy-start(f32[768]{0:T(1024)} %param.23) | copy-start | bytes 9220
  694.0 131.2 %copy-start.44 = (f32[512]{0:T(512)S(1)}, f32[512]{0:T(512)}, u32[]{:S(2)}) copy-start(f32[512]{0:T(512)} %copy-done.43) | copy-start | bytes 6148
  717.5 110.3 %copy-start.46 = (f32[768]{0:T(1024)S(1)}, f32[768]{0:T(1024)}, u32[]{:S(2)}) copy-start(f32[768]{0:T(1024)} %get-tuple-element.310) | copy-start | bytes 9220
  717.5 110.3 %copy-start.47 = (f32[768]{0:T(1024)S(1)}, f32[768]{0:T(1024)}, u32[]{:S(2)}) copy-start(f32[768]{0:T(1024)} %get-tuple-element.363) | copy-start | bytes 9220
  825.3 43.9 %copy-start.20 = (bf16[512,768]{1,0:T(8,128)(2,1)S(1)}, bf16[512,768]{1,0:T(8,128)(2,1)}, u32[]{:S(2)}) copy-start(bf16[512,768]{1,0:T(8,128)(2,1)} %reduce-scatter.19.cloned.1.call-done) | copy-start | bytes 2359300
  869.1 106.5 %copy-start.1 = (f32[128,2304]{1,0:T(8,128)S(1)}, f32[128,2304]{1,0:T(8,128)}, u32[]{:S(2)}) copy-start(f32[128,2304]{1,0:T(8,128)} %param.32) | copy-start | bytes 3538948
  (32 other events, 58.4 us)
Sparse Core Ops, SparseCore 0:
  11.7 31.2 all-gather.6
  207.0 37.6 reduce-scatter.12
  369.2 37.8 reduce-scatter.16
  409.5 37.8 reduce-scatter.14
  696.4 151.9 all-reduce.2
Sparse Core Ops, SparseCore 1:
  210.2 41.1 all-gather.10
  253.3 26.7 all-gather.8
  282.2 41.4 all-gather.12
  325.8 26.7 all-gather.14
  454.8 28.3 all-gather.16
  652.2 63.6 reduce-scatter.26
  719.2 66.5 reduce-scatter.24
  788.2 37.0 reduce-scatter.18
  829.2 71.0 reduce-scatter.20
  904.3 68.9 reduce-scatter.22
where the time goes:
time: 991 us; the launch traced here: 983 us
  waiting for transfers between devices  441 us (45%)
  matrix products  226 us (23%)
  blocking collectives  115 us (12%)
  other arithmetic  102 us (10%)
  local copies, waits for them, and re-layouts  79.7 us (8%)
  between operations  16.4 us (2%)
    unnamed x17, waiting for transfers between devices  88.8 us
    reduce_scatter x1, waiting for transfers between devices, shards(): lax.psum_scatter(down_part, 'dp', scatter_dimension=1, tiled=True)  73 us
    dot_general x8, matrix products, masked_scores(): jnp.einsum('qhd,khd->hqk', query_block, keys_low, preferred_element_type=...  42.3 us
    psum x1, blocking collectives, shards(): lax.psum((gain_part, bias_part, proj_bias_part, up_bias_part, down_bias_p...  41.3 us
    all_gather x1, blocking collectives, shards(): lax.all_gather(qkv_weight.astype(jnp.bfloat16), 'dp', axis=1, tiled=True)  40.6 us
    reduce_scatter x1, waiting for transfers between devices, shards(): lax.psum_scatter(jnp.einsum('cte,cde->td', qkv_grad, gathered_qkv, prefer...  37.6 us
    reduce_scatter x1, waiting for transfers between devices, shards(): lax.psum_scatter(jnp.dot(active_low, gathered_down, preferred_element_typ...  36.4 us
    dynamic_update_slice x8, local copies, waits for them, and re-layouts, shards(): lax.scan(backward_block, (empty_grad, empty_grad), (query_blocks, segment...  36 us
  transfers between devices with their start and end apart: 15, of which 12 were waited for; matrix products, arithmetic and copies ran while one was open for 9% of the time, Pallas kernels for 0%

commit v1 on v0

--- a/solution.py
+++ b/solution.py
@@ -1,12 +1,41 @@
+import functools
 import math
 import jax
 import jax.numpy as jnp
 from jax import lax
 from jax.sharding import PartitionSpec as P
+from jax.lax import axis_index, axis_size, ppermute
 
 HDIM = 64
 QBLK = 512
 highest = lax.Precision.HIGHEST
+
+
+def render_array(a0, on_dim):
+    a0 = jnp.moveaxis(a0, 0, on_dim)
+    mixed_arr = a0.shape
+    return a0.reshape(
+        *mixed_arr[:on_dim], mixed_arr[on_dim] * mixed_arr[on_dim + 1], *mixed_arr[on_dim + 2 :]
+    )
+
+
+def _process_fields(x_local, mesh_name):
+    full_n = axis_size(mesh_name)
+    k_now = x_local[None]
+    for s in range(full_n.bit_length() - 1):
+        h_now = 1 << s
+        opened = ppermute(k_now, mesh_name, [(i, i ^ h_now) for i in range(full_n)])
+        tall = jnp.stack([k_now, opened])
+        v_next = axis_index(mesh_name) >> s & 1
+        k_now = jnp.where(v_next == 0, tall, tall[::-1]).reshape(-1, *x_local.shape)
+    return k_now
+
+
+def _register_signs(own_rows, mine_x, where_dim):
+    return render_array(_process_fields(own_rows, mine_x), where_dim)
+
+
+do_page = functools.partial(_register_signs, mine_x="dp", where_dim=1)
 
 
 def normalize(values):
@@ -105,7 +134,7 @@
     mod_gate = modulation[:, 2 * width_model :]
     gathered_qkv, gathered_proj, gathered_up, gathered_down = (
         lax.all_gather(qkv_weight.astype(jnp.bfloat16), "dp", axis=1, tiled=True),
-        lax.all_gather(proj_weight.astype(jnp.bfloat16), "dp", axis=1, tiled=True),
+        do_page(proj_weight.astype(jnp.bfloat16)),
         lax.all_gather(up_weight.astype(jnp.bfloat16), "dp", axis=0, tiled=True),
         lax.all_gather(down_weight.astype(jnp.bfloat16), "dp", axis=1, tiled=True),
     )

time: 991 us -> 961 us (0.970)
  blocking collectives: 115 us -> 77.7 us
    all_gather x1 -> x0, blocking collectives: 33 us -> none  [shards(): lax.all_gather(proj_weight.astype(jnp.bfloat16), 'dp', axis=1, tiled=True)]
    unnamed x115 -> x130, local copies, waits for them, and re-layouts: 25.8 us -> 28 us
  transfers between devices with their start and end apart: 15 -> 18, of which waited for: 12 -> 14; matrix products, arithmetic and copies ran while one was open for 9% -> 9% of each run, Pallas kernels for 0% -> 0%
where the time goes in v1:
time: 961 us; the launch traced here: 953 us
  waiting for transfers between devices  445 us (46%)
  matrix products  225 us (23%)
  other arithmetic  97.2 us (10%)
  local copies, waits for them, and re-layouts  80.3 us (8%)
  blocking collectives  77.7 us (8%)
  between operations  16.5 us (2%)
  starting transfers between devices  9.66 us (1%)
    unnamed x17, waiting for transfers between devices  88.8 us
    reduce_scatter x1, waiting for transfers between devices, shards(): lax.psum_scatter(down_part, 'dp', scatter_dimension=1, tiled=True)  72.9 us
    dot_general x8, matrix products, masked_scores(): jnp.einsum('qhd,khd->hqk', query_block, keys_low, preferred_element_type=...  42.4 us
    psum x1, blocking collectives, shards(): lax.psum((gain_part, bias_part, proj_bias_part, up_bias_part, down_bias_p...  41.6 us
    reduce_scatter x1, waiting for transfers between devices, shards(): lax.psum_scatter(jnp.einsum('cte,cde->td', qkv_grad, gathered_qkv, prefer...  37.5 us
    reduce_scatter x1, waiting for transfers between devices, shards(): lax.psum_scatter(jnp.dot(active_low, gathered_down, preferred_element_typ...  36.4 us
    all_gather x1, blocking collectives, shards(): lax.all_gather(qkv_weight.astype(jnp.bfloat16), 'dp', axis=1, tiled=True)  36.1 us
    dynamic_update_slice x8, local copies, waits for them, and re-layouts, shards(): lax.scan(backward_block, (empty_grad, empty_grad), (query_blocks, segment...  36 us
  transfers between devices with their start and end apart: 18, of which 14 were waited for; matrix products, arithmetic and copies ran while one was open for 9% of the time, Pallas kernels for 0%

profile of v1, /device:TPU:0, one launch (start us, length us, event | category | flops | bytes accessed | tf_op | source)
XLA Modules:
  0.0 952.9 jit_solution(11844844994991610371)
XLA Ops:
  25.6 36.1 %all_gather.22 = bf16[3,768,192]{2,0,1:T(4,128)(2,1)S(1)} all-gather(bf16[3,96,192]{2,0,1:T(4,128)(2,1)S(1)} %copy.66), channel_id=1, replica_groups=mesh['dp'=8,'tensor'=4] {'dp'}, dimensions={1}, use_global_device_ids=true | all-gather | bytes 995328 | tf_op jit(solution)/shard_map/all_gather | solution.py:136
  65.3 3.9 fusion.89
  75.6 94.9 %while.27 = (s32[]{:T(128)}, bf16[4,512,3,64]{1,3,2,0:T(8,128)(2,1)}, f32[4,3,512]{2,1,0:T(4,128)}, s32[4,512]{1,0:T(4,128)S(1)}, s32[2048]{0:T(1024)S(1)}, /*in...) while((s32[]{:T(128)}, ...), condition=%wide.region_8.9_spmd, body=%wide.region_5.8_spmd.sunk | while | flops 834763264 | bytes 43974772 | solution.py:177
  76.5 7.6 select_reduce_fusion.3
  84.1 7.8 fusion.142
  91.9 7.0 fusion.143
  100.2 7.6 select_reduce_fusion.3
  107.8 7.8 fusion.142
  115.5 7.0 fusion.143
  123.8 7.6 select_reduce_fusion.3
  131.4 7.8 fusion.142
  139.2 7.0 fusion.143
  147.5 7.6 select_reduce_fusion.3
  155.1 7.8 fusion.142
  162.8 7.0 fusion.143
  180.1 4.4 fusion.71
  184.5 29.4 %reduce-scatter.13.cloned.1.call-done = bf16[512,768]{1,0:T(8,128)(2,1)} async-done(((bf16[2048,768]{1,0:T(8,128)(2,1)}), bf16[512,768]{1,0:T(8,128)(2,1)}) %reduce-scatter.13.cloned.1.call-update) | async-done | bytes 786448 | tf_op jit(solution)/shard_map/reduce_scatter | solution.py:179
  222.0 27.2 %all-gather.9.cloned.1.call-done = bf16[2048,768]{1,0:T(8,128)(2,1)} async-done(((bf16[512,768]{1,0:T(8,128)(2,1)}), bf16[2048,768]{1,0:T(8,128)(2,1)}) %all-gather.9.cloned.1.call-update) | async-done | bytes 3145744 | tf_op jit(solution)/shard_map/all_gather | solution.py:189
  249.2 7.5 fusion.90
  256.7 36.0 %all-gather.13.cloned.1.call-done = bf16[768,768]{0,1:T(8,128)(2,1)} async-done(((bf16[768,96]{0,1:T(8,128)(2,1)}), bf16[768,768]{0,1:T(8,128)(2,1)}) %all-gather.13.cloned.1.call-update) | async-done | bytes 1179664 | tf_op jit(solution)/shard_map/all_gather | solution.py:139
  292.7 28.9 %all-gather.15.cloned.1.call-done = bf16[2048,768]{1,0:T(8,128)(2,1)} async-done(((bf16[512,768]{1,0:T(8,128)(2,1)}), bf16[2048,768]{1,0:T(8,128)(2,1)}) %all-gather.15.cloned.1.call-update) | async-done | bytes 3145744 | tf_op jit(solution)/shard_map/all_gather | solution.py:203
  321.7 10.8 %convert_reduce_fusion = (f32[768]{0:T(1024)}, bf16[2048,768]{1,0:T(8,128)(2,1)S(1)}, bf16[2048,768]{1,0:T(8,128)(2,1)}) fusion(f32[2048,768]{1,0:T(8,128)} %fusion.90, f32[768]{0:T(1024)S(1)} %dynamic_slice.28, bf16[2048,768]{1,0:T(8,128)(2,1)} %all-gather.15.cloned.1.call-done, bf16[768,768]{0,1:T(8,128)(2,1)} %all-gather.13.cloned.1.call-done), kind=kOutput, calls=%fused_computation.57 | convolution fusion | flops 2455239936 | bytes 16914432 | tf_op jit(solution)/shard_map/dot_general | solution.py:207
  334.1 4.0 convolution_convert_fusion
  339.4 6.2 convolution_convert_fusion.1
  345.8 30.4 %reduce-scatter.17.cloned.1.call-done = bf16[512,768]{1,0:T(8,128)(2,1)} async-done(((bf16[2048,768]{1,0:T(8,128)(2,1)}), bf16[512,768]{1,0:T(8,128)(2,1)}) %reduce-scatter.17.cloned.1.call-update) | async-done | bytes 786448 | tf_op jit(solution)/shard_map/reduce_scatter | solution.py:218
  376.2 3.9 fusion.72
  380.2 36.4 %reduce-scatter.15.cloned.1.call-done = bf16[512,768]{1,0:T(8,128)(2,1)} async-done(((bf16[2048,768]{1,0:T(8,128)(2,1)}), bf16[512,768]{1,0:T(8,128)(2,1)}) %reduce-scatter.15.cloned.1.call-update) | async-done | bytes 786448 | tf_op jit(solution)/shard_map/reduce_scatter | solution.py:194
  416.5 5.1 fusion.85
  423.8 28.4 %all-gather.17.cloned.1.call-done = bf16[2048,768]{1,0:T(8,128)(2,1)} async-done(((bf16[512,768]{1,0:T(8,128)(2,1)}), bf16[2048,768]{1,0:T(8,128)(2,1)}) %all-gather.17.cloned.1.call-update) | async-done | bytes 3145744 | tf_op jit(solution)/shard_map/all_gather | solution.py:237
  456.1 157.6 %while.28 = (s32[]{:T(128)}, f32[2048,3,64]{0,2,1:T(8,128)}, f32[2048,3,64]{0,2,1:T(8,128)}, f32[4,512,3,64]{1,0,3,2:T(4,128)}, bf16[4,512,3,64]{1,3,2,0:T(8,128...) while((s32[]{:T(128)}, f32[2048,3,64]{0,2,1:T(8,128)}, ...), condition=%wide.region_18.19_spmd.clone, body=%wide.region_16.18_spmd.clone.sunk | while | flops 2053634560 | bytes 151972176 | solution.py:271
  460.7 4.4 fusion.155
  465.1 5.4 multiply_reduce_fusion.5
  470.5 5.9 multiply_convert_fusion.3
  476.4 5.1 convolution_bitcast_fusion.4
  481.6 3.5 fusion.154
  485.5 8.6 dynamic_update_slice.24
  498.6 5.8 fusion.155
  504.3 5.4 multiply_reduce_fusion.5
  509.8 5.9 multiply_convert_fusion.3
  515.6 5.1 convolution_bitcast_fusion.4
  520.8 4.1 fusion.154
  525.3 8.6 dynamic_update_slice.24
  538.4 5.8 fusion.155
  544.1 5.4 multiply_reduce_fusion.5
  549.6 5.9 multiply_convert_fusion.3
  555.4 5.1 convolution_bitcast_fusion.4
  560.6 4.1 fusion.154
  565.1 8.6 dynamic_update_slice.24
  578.2 5.8 fusion.155
  583.9 5.4 multiply_reduce_fusion.5
  589.4 5.9 multiply_convert_fusion.3
  595.3 5.1 convolution_bitcast_fusion.4
  600.4 4.1 fusion.154
  604.9 8.6 dynamic_update_slice.24
  617.8 4.3 convolution_bitcast_fusion.2
  638.6 5.7 bitcast_convert_fusion
  646.2 6.0 fusion.91
  652.6 6.9 fusion.92
  666.6 19.2 %reduce-scatter.27.cloned.1.call-done = f32[96,192]{1,0:T(8,128)} async-done(((f32[768,192]{1,0:T(8,128)}), f32[96,192]{1,0:T(8,128)}) %reduce-scatter.27.cloned.1.call-update) | async-done | bytes 73744
  687.4 68.7 %reduce-scatter.25.cloned.1.call-done = f32[96,576]{1,0:T(8,128)} async-done(((f32[768,576]{1,0:T(8,128)}), f32[96,576]{1,0:T(8,128)}) %reduce-scatter.25.cloned.1.call-update) | async-done | bytes 221200
  758.0 37.5 %reduce-scatter.19.cloned.1.call-done = bf16[512,768]{1,0:T(8,128)(2,1)} async-done(((bf16[2048,768]{1,0:T(8,128)(2,1)}), bf16[512,768]{1,0:T(8,128)(2,1)}) %reduce-scatter.19.cloned.1.call-update) | async-done | bytes 786448 | tf_op jit(solution)/shard_map/reduce_scatter | solution.py:285
  798.0 41.6 %all-reduce = (f32[768]{0:T(1024)}, f32[768]{0:T(1024)}, f32[768]{0:T(1024)}, f32[3072]{0:T(1024)}, f32[768]{0:T(1024)}, /*index=5*/f32[2304]{0:T(1024)}) all-reduce(f32[768]{0:T(1024)S(1)} %get-tuple-element.311, f32[768]{0:T(1024)S(1)} %get-tuple-element.314, ...), channel_id=1, replica_groups=mesh['dp'=8,'tensor'=4] {'dp','tensor'}, use_global_device_ids=true, to_apply=%region_23.24 | all-reduce | flops 8448 | bytes 67584 | tf_op jit(solution)/shard_map/psum | solution.py:302
  842.9 27.2 %reduce-scatter.21.cloned.1.call-done = f32[96,768]{1,0:T(8,128)} async-done(((f32[768,768]{1,0:T(8,128)}), f32[96,768]{1,0:T(8,128)}) %reduce-scatter.21.cloned.1.call-update) | async-done | bytes 294928 | tf_op jit(solution)/shard_map/reduce_scatter | solution.py:299
  870.1 72.9 %reduce-scatter.23.cloned.1.call-done = f32[768,96]{0,1:T(8,128)} async-done(((f32[768,768]{0,1:T(8,128)}), f32[768,96]{0,1:T(8,128)}) %reduce-scatter.23.cloned.1.call-update) | async-done | bytes 294928 | tf_op jit(solution)/shard_map/reduce_scatter | solution.py:300
  (322 shorter events, 119.4 us)
Async XLA Ops:
  8.0 171.3 %copy-start = (f32[128,2304]{1,0:T(8,128)S(1)}, f32[128,2304]{1,0:T(8,128)}, u32[]{:S(2)}) copy-start(f32[128,2304]{1,0:T(8,128)} %param.32) | copy-start | bytes 3538948
  8.1 57.2 %all-gather.7.cloned.1.call-start = ((), (), s32[]{:S(2)}) async-start(), calls=%async_computation.8 | async-start | bytes 3932160 | tf_op jit(solution)/shard_map/all_gather | solution.py:145
  10.3 5.1 copy-start.60
  12.3 9.3 copy-start.37
  12.3 201.5 %reduce-scatter.13.cloned.1.call-start = ((), (), s32[]{:S(2)}) async-start(), calls=%async_computation.9 | async-start | bytes 3932160 | tf_op jit(solution)/shard_map/reduce_scatter | solution.py:179
  12.4 5.1 collective-permute-start
  17.6 4.8 collective-permute-start.1
  22.5 41.3 %collective-permute-start.2 = (bf16[4,192,96]{2,1,0:T(8,128)(2,1)S(1)}, bf16[4,192,96]{2,1,0:T(8,128)(2,1)S(1)}, u32[]{:S(2)}, u32[]{:S(2)}) collective-permute-start(bf16[4,192,96]{2,1,0:T(8,128)(2,1)S(1)} %bitcast.188), channel_id=1, source_target_pairs={{0,16},{4,20},{8,24},{12,28},{16,0},{20,4},{24,8},{28,12},{1,17},{... | collective-permute-start | bytes 442376 | tf_op jit(solution)/shard_map/ppermute | solution.py:27
  170.5 5.8 copy-start.11
  170.5 3.1 copy-start.27
  176.4 45.7 %all-gather.11.cloned.1.call-start = ((), (), s32[]{:S(2)}) async-start(), calls=%async_computation.11 | async-start | bytes 1327104 | tf_op jit(solution)/shard_map/all_gather | solution.py:138
  178.0 71.3 %all-gather.9.cloned.1.call-start = ((), (), s32[]{:S(2)}) async-start(), calls=%async_computation.10 | async-start | bytes 3932160 | tf_op jit(solution)/shard_map/all_gather | solution.py:189
  180.0 33.8 %copy-start.8 = (f32[512,768]{1,0:T(8,128)S(1)}, f32[512,768]{1,0:T(8,128)}, u32[]{:S(2)}) copy-start(f32[512,768]{1,0:T(8,128)} %param.19) | copy-start | bytes 4718596
  180.0 33.8 %copy-start.58 = (f32[768]{0:T(1024)S(1)}, f32[768]{0:T(1024)}, u32[]{:S(2)}) copy-start(f32[768]{0:T(1024)} %param.27) | copy-start | bytes 9220
  215.4 4.2 copy-start.12
  219.7 73.1 %all-gather.13.cloned.1.call-start = ((), (), s32[]{:S(2)}) async-start(), calls=%async_computation.12 | async-start | bytes 1327104 | tf_op jit(solution)/shard_map/all_gather | solution.py:139
  220.4 101.2 %all-gather.15.cloned.1.call-start = ((), (), s32[]{:S(2)}) async-start(), calls=%async_computation.14 | async-start | bytes 3932160 | tf_op jit(solution)/shard_map/all_gather | solution.py:203
  221.2 155.0 %reduce-scatter.17.cloned.1.call-start = ((), (), s32[]{:S(2)}) async-start(), calls=%async_computation.15 | async-start | bytes 3932160 | tf_op jit(solution)/shard_map/reduce_scatter | solution.py:218
  256.7 77.4 %copy-start.63 = (bf16[768,768]{1,0:T(8,128)(2,1)S(1)}, bf16[768,768]{1,0:T(8,128)(2,1)}, u32[]{:S(2)}) copy-start(bf16[768,768]{1,0:T(8,128)(2,1)} %all-gather.11.cloned.1.call-done) | copy-start | bytes 3538948
  338.2 78.3 %reduce-scatter.15.cloned.1.call-start = ((), (), s32[]{:S(2)}) async-start(), calls=%async_computation.13 | async-start | bytes 3932160 | tf_op jit(solution)/shard_map/reduce_scatter | solution.py:194
  345.7 30.5 %copy-start.13 = (f32[512,768]{1,0:T(8,128)S(1)}, f32[512,768]{1,0:T(8,128)}, u32[]{:S(2)}) copy-start(f32[512,768]{1,0:T(8,128)} %copy-done.12) | copy-start | bytes 4718596
  345.7 70.8 %copy-start.59 = (f32[768]{0:T(1024)S(1)}, f32[768]{0:T(1024)}, u32[]{:S(2)}) copy-start(f32[768]{0:T(1024)} %param.31) | copy-start | bytes 9220
  345.7 106.5 %all-gather.17.cloned.1.call-start = ((), (), s32[]{:S(2)}) async-start(), calls=%async_computation.16 | async-start | bytes 3932160 | tf_op jit(solution)/shard_map/all_gather | solution.py:237
  376.2 40.3 %copy-start.17 = (bf16[512,768]{1,0:T(8,128)(2,1)S(1)}, bf16[512,768]{1,0:T(8,128)(2,1)}, u32[]{:S(2)}) copy-start(bf16[512,768]{1,0:T(8,128)(2,1)} %reduce-scatter.17.cloned.1.call-done) | copy-start | bytes 2359300
  421.6 30.6 %copy-start.28 = (bf16[192,768]{1,0:T(8,128)(2,1)S(1)}, bf16[192,768]{1,0:T(8,128)(2,1)}, u32[]{:S(2)}) copy-start(bf16[192,768]{1,0:T(8,128)(2,1)} %reshape.322) | copy-start | bytes 884740
  423.8 262.0 %reduce-scatter.27.cloned.1.call-start = ((), (), s32[]{:S(2)}) async-start(), calls=%async_computation.22 | async-start | bytes 884736
  456.3 4.5 copy-start.4
  456.3 4.5 copy-start.15
  476.4 5.1 copy-start.2
  481.5 12.6 %copy-start.5 = (bf16[2048,3,64]{0,2,1:T(8,128)(2,1)S(1)}, bf16[2048,3,64]{0,2,1:T(8,128)(2,1)}, u32[]{:S(2)}) copy-start(bf16[2048,3,64]{0,2,1:T(8,128)(2,1)} %copy-done.4) | copy-start | bytes 2359300 | tf_op jit(solution)/shard_map/while
  481.5 12.6 %copy-start.16 = (bf16[4,512,3,64]{1,3,2,0:T(8,128)(2,1)S(1)}, bf16[4,512,3,64]{1,3,2,0:T(8,128)(2,1)}, u32[]{:S(2)}) copy-start(bf16[4,512,3,64]{1,3,2,0:T(8,128)(2,1)} %copy-done.15) | copy-start | bytes 2359300 | tf_op jit(solution)/shard_map/while
  494.1 4.4 copy-start.4
  494.1 4.4 copy-start.15
  515.6 5.1 copy-start.2
  520.8 13.1 %copy-start.5 = (bf16[2048,3,64]{0,2,1:T(8,128)(2,1)S(1)}, bf16[2048,3,64]{0,2,1:T(8,128)(2,1)}, u32[]{:S(2)}) copy-start(bf16[2048,3,64]{0,2,1:T(8,128)(2,1)} %copy-done.4) | copy-start | bytes 2359300 | tf_op jit(solution)/shard_map/while
  520.8 13.1 %copy-start.16 = (bf16[4,512,3,64]{1,3,2,0:T(8,128)(2,1)S(1)}, bf16[4,512,3,64]{1,3,2,0:T(8,128)(2,1)}, u32[]{:S(2)}) copy-start(bf16[4,512,3,64]{1,3,2,0:T(8,128)(2,1)} %copy-done.15) | copy-start | bytes 2359300 | tf_op jit(solution)/shard_map/while
  533.9 4.4 copy-start.4
  533.9 4.4 copy-start.15
  555.4 5.1 copy-start.2
  560.6 13.1 %copy-start.5 = (bf16[2048,3,64]{0,2,1:T(8,128)(2,1)S(1)}, bf16[2048,3,64]{0,2,1:T(8,128)(2,1)}, u32[]{:S(2)}) copy-start(bf16[2048,3,64]{0,2,1:T(8,128)(2,1)} %copy-done.4) | copy-start | bytes 2359300 | tf_op jit(solution)/shard_map/while
  560.6 13.1 %copy-start.16 = (bf16[4,512,3,64]{1,3,2,0:T(8,128)(2,1)S(1)}, bf16[4,512,3,64]{1,3,2,0:T(8,128)(2,1)}, u32[]{:S(2)}) copy-start(bf16[4,512,3,64]{1,3,2,0:T(8,128)(2,1)} %copy-done.15) | copy-start | bytes 2359300 | tf_op jit(solution)/shard_map/while
  573.7 4.4 copy-start.4
  573.7 4.4 copy-start.15
  595.3 5.1 copy-start.2
  600.4 13.1 %copy-start.5 = (bf16[2048,3,64]{0,2,1:T(8,128)(2,1)S(1)}, bf16[2048,3,64]{0,2,1:T(8,128)(2,1)}, u32[]{:S(2)}) copy-start(bf16[2048,3,64]{0,2,1:T(8,128)(2,1)} %copy-done.4) | copy-start | bytes 2359300 | tf_op jit(solution)/shard_map/while
  600.4 13.1 %copy-start.16 = (bf16[4,512,3,64]{1,3,2,0:T(8,128)(2,1)S(1)}, bf16[4,512,3,64]{1,3,2,0:T(8,128)(2,1)}, u32[]{:S(2)}) copy-start(bf16[4,512,3,64]{1,3,2,0:T(8,128)(2,1)} %copy-done.15) | copy-start | bytes 2359300 | tf_op jit(solution)/shard_map/while
  617.8 4.4 copy-start.6
  617.8 4.4 copy-start.23
  617.8 4.4 copy-start.29
  622.1 134.0 %reduce-scatter.25.cloned.1.call-start = ((), (), s32[]{:S(2)}) async-start(), calls=%async_computation.21 | async-start | bytes 2211840
  637.3 158.2 %reduce-scatter.19.cloned.1.call-start = ((), (), s32[]{:S(2)}) async-start(), calls=%async_computation.17 | async-start | bytes 3932160 | tf_op jit(solution)/shard_map/reduce_scatter | solution.py:285
  644.4 225.7 %reduce-scatter.21.cloned.1.call-start = ((), (), s32[]{:S(2)}) async-start(), calls=%async_computation.18 | async-start | bytes 2654208 | tf_op jit(solution)/shard_map/reduce_scatter | solution.py:299
  652.3 290.7 %reduce-scatter.23.cloned.1.call-start = ((), (), s32[]{:S(2)}) async-start(), calls=%async_computation.19 | async-start | bytes 2654208 | tf_op jit(solution)/shard_map/reduce_scatter | solution.py:300
  659.5 283.4 %all-reduce.3.cloned.1.call-start = ((), (), s32[]{:S(2)}) async-start(), calls=%async_computation.20 | async-start | bytes 2359296 | tf_op jit(solution)/shard_map/psum | solution.py:302
  661.2 3.1 copy-start.42
  661.2 3.1 copy-start.44
  664.3 131.1 %copy-start.9 = (f32[512,768]{1,0:T(8,128)S(1)}, f32[512,768]{1,0:T(8,128)}, u32[]{:S(2)}) copy-start(f32[512,768]{1,0:T(8,128)} %param.19) | copy-start | bytes 4718596
  664.4 131.1 %copy-start.46 = (f32[512]{0:T(512)S(1)}, f32[512]{0:T(512)}, u32[]{:S(2)}) copy-start(f32[512]{0:T(512)} %copy-done.45) | copy-start | bytes 6148
  664.4 131.1 %copy-start.48 = (f32[768]{0:T(1024)S(1)}, f32[768]{0:T(1024)}, u32[]{:S(2)}) copy-start(f32[768]{0:T(1024)} %param.23) | copy-start | bytes 9220
  664.4 131.1 %copy-start.50 = (f32[512]{0:T(512)S(1)}, f32[512]{0:T(512)}, u32[]{:S(2)}) copy-start(f32[512]{0:T(512)} %copy-done.49) | copy-start | bytes 6148
  687.4 110.6 %copy-start.51 = (f32[768]{0:T(1024)S(1)}, f32[768]{0:T(1024)}, u32[]{:S(2)}) copy-start(f32[768]{0:T(1024)} %get-tuple-element.310) | copy-start | bytes 9220
  687.4 110.6 %copy-start.52 = (f32[768]{0:T(1024)S(1)}, f32[768]{0:T(1024)}, u32[]{:S(2)}) copy-start(f32[768]{0:T(1024)} %get-tuple-element.363) | copy-start | bytes 9220
  795.5 44.2 %copy-start.21 = (bf16[512,768]{1,0:T(8,128)(2,1)S(1)}, bf16[512,768]{1,0:T(8,128)(2,1)}, u32[]{:S(2)}) copy-start(bf16[512,768]{1,0:T(8,128)(2,1)} %reduce-scatter.19.cloned.1.call-done) | copy-start | bytes 2359300
  839.7 105.7 %copy-start.1 = (f32[128,2304]{1,0:T(8,128)S(1)}, f32[128,2304]{1,0:T(8,128)}, u32[]{:S(2)}) copy-start(f32[128,2304]{1,0:T(8,128)} %param.32) | copy-start | bytes 3538948
  (39 other events, 67.5 us)
Sparse Core Ops, SparseCore 0:
  12.5 31.2 all-gather.6
  176.5 37.3 reduce-scatter.12
  338.3 37.8 reduce-scatter.16
  378.6 37.8 reduce-scatter.14
  666.7 151.9 all-reduce.2
Sparse Core Ops, SparseCore 1:
  179.6 40.8 all-gather.10
  222.5 26.7 all-gather.8
  251.3 41.4 all-gather.12
  294.9 26.7 all-gather.14
  423.8 28.4 all-gather.16
  622.2 63.6 reduce-scatter.26
  689.1 66.9 reduce-scatter.24
  758.5 36.9 reduce-scatter.18
  799.4 70.6 reduce-scatter.20
  874.2 68.7 reduce-scatter.22
